TPU v7x, 32 devices: a whole 2x2x4 slice. The times are simulated.
32 devices in a mesh: dp: 8 (over z, x), mp: 4 (over y, core).
Axes of the slice: x: 2, y: 2, z: 4, core: 2. Of those that a mesh axis runs over, the one named last changes fastest.
Arguments:
- tokens: bfloat16 [16384, 1024], P('dp'), may hold values from -6 to 6
- cotangent: bfloat16 [16384, 1024], P('dp'), may hold values from -15 to 15
- item_lengths: int32 [8, 8], P('dp'), may hold values from 1 to 1024, 2048 in all within a row
- w_qkv: bfloat16 [3, 1024, 1024], P(None, None, 'mp'), may hold values from -0.1875 to 0.1875
- b_qv: float32 [2, 1024], P(None, 'mp'), may hold values from -3 to 3
- w_out: bfloat16 [1024, 1024], P('mp'), may hold values from -0.75 to 0.75
- b_out: float32 [1024], replicated, may hold values from -1.75 to 1.75
- w_fc1: bfloat16 [1024, 4096], P(None, 'mp'), may hold values from -0.1875 to 0.1875
- b_fc1: float32 [4096], P('mp'), may hold values from -3 to 3
- w_fc2: bfloat16 [4096, 1024], P('mp'), may hold values from -0.09375 to 0.09375
- b_fc2: float32 [1024], replicated, may hold values from -1.75 to 1.75
- ln1_gain: float32 [1024], replicated, may hold values from 0.5 to 1.5
- ln1_bias: float32 [1024], replicated, may hold values from -1.75 to 1.75
- ln2_gain: float32 [1024], replicated, may hold values from 0.5 to 1.5
- ln2_bias: float32 [1024], replicated, may hold values from -1.75 to 1.75
Outputs:
- output: bfloat16 [16384, 1024], P('dp')
- grad_tokens: float32 [16384, 1024], P('dp')
- grad_w_qkv: float32 [3, 1024, 1024], P(None, 'dp', 'mp')
- grad_b_qv: float32 [2, 1024], P(None, 'mp')
- grad_w_out: float32 [1024, 1024], P('mp', 'dp')
- grad_b_out: float32 [1024], replicated
- grad_w_fc1: float32 [1024, 4096], P('dp', 'mp')
- grad_b_fc1: float32 [4096], P('mp')
- grad_w_fc2: float32 [4096, 1024], P('mp', 'dp')
- grad_b_fc2: float32 [1024], replicated
- grad_ln1_gain: float32 [1024], replicated
- grad_ln1_bias: float32 [1024], replicated
- grad_ln2_gain: float32 [1024], replicated
- grad_ln2_bias: float32 [1024], replicated
Inputs may be any that keep to these rules, and one draw needn't show every extreme that they name: `item_lengths`: each row sums to 2048, and each row's longest item has exactly 1024 patches.
All inputs are finite; a program needn't handle non-finite values.
Results may differ from a plain program's by a relative error of at most 0.019.
Values may be sent and summed in bfloat16 or wider, within the bound.
A program may use at most 192 MiB of HBM per device.

v0:
```python
from functools import partial
import jax
import jax.numpy as jnp
from jax import lax
from jax.sharding import PartitionSpec as P

HEAD = 64
QBLOCK = 512


def normalize(values, gain, shift):
    center = jnp.mean(values, axis=-1, keepdims=True)
    centered = values - center
    spread = jnp.mean(centered * centered, axis=-1, keepdims=True)
    return centered * lax.rsqrt(spread + 1e-06) * gain + shift


def exact_gelu(values):
    return jax.nn.gelu(values, approximate=False)


def segment_ids(lengths_row, row_count):
    ends = jnp.cumsum(lengths_row)
    positions = jnp.arange(row_count, dtype=jnp.int32)
    return jnp.sum((positions[:, None] >= ends[None, :]).astype(jnp.int32), axis=1)


def mp_allreduce(partial, n_mp):
    if n_mp != 4:
        return lax.psum(partial, "mp").astype(jnp.float32)
    idx = lax.axis_index("mp")
    low_bit = idx % 2
    half = partial.shape[0] // 2
    mine = lax.dynamic_slice_in_dim(partial, low_bit * half, half, 0)
    other = lax.dynamic_slice_in_dim(partial, (1 - low_bit) * half, half, 0)
    got = lax.ppermute(other, "mp", [(k, k ^ 1) for k in range(4)])
    first = (mine.astype(jnp.float32) + got.astype(jnp.float32)).astype(jnp.bfloat16)
    got_far = lax.ppermute(first, "mp", [(k, k ^ 2) for k in range(4)])
    second = (first.astype(jnp.float32) + got_far.astype(jnp.float32)).astype(jnp.bfloat16)
    got_back = lax.ppermute(second, "mp", [(k, k ^ 1) for k in range(4)])
    top = jnp.where(low_bit == 0, second, got_back)
    bottom = jnp.where(low_bit == 0, got_back, second)
    return jnp.concatenate([top, bottom], axis=0).astype(jnp.float32)


def per_device(
    n_mp,
    tokens,
    cotangent,
    item_lengths,
    w_qkv,
    b_qv,
    w_out,
    b_out,
    w_fc1,
    b_fc1,
    w_fc2,
    b_fc2,
    ln1_gain,
    ln1_bias,
    ln2_gain,
    ln2_bias,
):
    row_count = tokens.shape[0]
    local_cols = w_qkv.shape[2]
    heads_here = local_cols // HEAD
    blocks = row_count // QBLOCK
    score_scale = HEAD ** (-0.5)
    segments = segment_ids(item_lengths[0], row_count)
    seg_blocks = segments.reshape(blocks, QBLOCK)
    inputs = tokens.astype(jnp.float32)
    norm_one, norm_one_back = jax.vjp(normalize, inputs, ln1_gain, ln1_bias)
    normed_one = norm_one.astype(jnp.bfloat16)
    queries = (jnp.dot(normed_one, w_qkv[0], preferred_element_type=jnp.float32) + b_qv[0]).astype(
        jnp.bfloat16
    )
    key_rows = jnp.dot(normed_one, w_qkv[1], preferred_element_type=jnp.float32).astype(
        jnp.bfloat16
    )
    value_rows = (
        jnp.dot(normed_one, w_qkv[2], preferred_element_type=jnp.float32) + b_qv[1]
    ).astype(jnp.bfloat16)
    key_heads = key_rows.reshape(row_count, heads_here, HEAD)
    value_heads = value_rows.reshape(row_count, heads_here, HEAD)
    query_blocks = queries.reshape(blocks, QBLOCK, heads_here, HEAD)

    def block_scores(query_block, seg_block):
        scores = (
            jnp.einsum("qhd,khd->hqk", query_block, key_heads, preferred_element_type=jnp.float32)
            * score_scale
        )
        same = seg_block[:, None] == segments[None, :]
        return jnp.where(same[None], scores, -1e30)

    def forward_block(pieces):
        query_block, seg_block = pieces
        scores = block_scores(query_block, seg_block)
        row_max = jnp.max(scores, axis=-1, keepdims=True)
        raised = jnp.exp(scores - row_max)
        row_sum = jnp.sum(raised, axis=-1, keepdims=True)
        probs = raised / row_sum
        block_out = jnp.einsum(
            "hqk,khd->qhd",
            probs.astype(jnp.bfloat16),
            value_heads,
            preferred_element_type=jnp.float32,
        )
        return (block_out.astype(jnp.bfloat16), (row_max + jnp.log(row_sum))[..., 0])

    out_blocks, log_norms = lax.map(forward_block, (query_blocks, seg_blocks))
    attended = out_blocks.reshape(row_count, local_cols)
    attention_sum = mp_allreduce(
        jnp.dot(attended, w_out, preferred_element_type=jnp.float32).astype(jnp.bfloat16), n_mp
    )
    middle = inputs + attention_sum + b_out
    norm_two, norm_two_back = jax.vjp(normalize, middle, ln2_gain, ln2_bias)
    normed_two = norm_two.astype(jnp.bfloat16)
    hidden_pre = jnp.dot(normed_two, w_fc1, preferred_element_type=jnp.float32) + b_fc1
    activated_full, gelu_back = jax.vjp(exact_gelu, hidden_pre)
    activated = activated_full.astype(jnp.bfloat16)
    mlp_sum = mp_allreduce(
        jnp.dot(activated, w_fc2, preferred_element_type=jnp.float32).astype(jnp.bfloat16), n_mp
    )
    output = (middle + mlp_sum + b_fc2).astype(jnp.bfloat16)
    upstream = cotangent.astype(jnp.float32)
    grad_b_fc2 = jnp.sum(upstream, axis=0)
    grad_w_fc2 = jnp.einsum("tf,td->fd", activated, cotangent, preferred_element_type=jnp.float32)
    d_act = jnp.einsum("td,fd->tf", cotangent, w_fc2, preferred_element_type=jnp.float32)
    d_pre = gelu_back(d_act)[0]
    grad_b_fc1 = jnp.sum(d_pre, axis=0)
    d_pre_low = d_pre.astype(jnp.bfloat16)
    grad_w_fc1 = jnp.einsum("td,tf->df", normed_two, d_pre_low, preferred_element_type=jnp.float32)
    d_normed_two = mp_allreduce(
        jnp.einsum("tf,df->td", d_pre_low, w_fc1, preferred_element_type=jnp.float32).astype(
            jnp.bfloat16
        ),
        n_mp,
    )
    d_middle_norm, grad_ln2_gain, grad_ln2_bias = norm_two_back(d_normed_two)
    d_middle = upstream + d_middle_norm
    grad_b_out = jnp.sum(d_middle, axis=0)
    d_middle_low = d_middle.astype(jnp.bfloat16)
    grad_w_out = jnp.einsum("tc,td->cd", attended, d_middle_low, preferred_element_type=jnp.float32)
    d_attended = jnp.einsum(
        "td,cd->tc", d_middle_low, w_out, preferred_element_type=jnp.float32
    ).astype(jnp.bfloat16)
    d_att_blocks = d_attended.reshape(blocks, QBLOCK, heads_here, HEAD)

    def backward_block(running, pieces):
        d_keys_acc, d_values_acc = running
        query_block, seg_block, d_out_block, log_norm = pieces
        scores = block_scores(query_block, seg_block)
        probs = jnp.exp(scores - log_norm[..., None])
        d_probs = jnp.einsum(
            "qhd,khd->hqk", d_out_block, value_heads, preferred_element_type=jnp.float32
        )
        d_scores = probs * (d_probs - jnp.sum(probs * d_probs, axis=-1, keepdims=True))
        d_scores_low = d_scores.astype(jnp.bfloat16)
        d_query_block = (
            jnp.einsum("hqk,khd->qhd", d_scores_low, key_heads, preferred_element_type=jnp.float32)
            * score_scale
        )
        d_keys_acc = (
            d_keys_acc
            + jnp.einsum(
                "hqk,qhd->khd", d_scores_low, query_block, preferred_element_type=jnp.float32
            )
            * score_scale
        )
        d_values_acc = d_values_acc + jnp.einsum(
            "hqk,qhd->khd",
            probs.astype(jnp.bfloat16),
            d_out_block,
            preferred_element_type=jnp.float32,
        )
        return ((d_keys_acc, d_values_acc), d_query_block)

    zeros_acc = jnp.zeros((row_count, heads_here, HEAD), jnp.float32)
    (d_keys, d_values), d_query_blocks = lax.scan(
        backward_block, (zeros_acc, zeros_acc), (query_blocks, seg_blocks, d_att_blocks, log_norms)
    )
    d_queries = d_query_blocks.reshape(row_count, local_cols)
    d_keys = d_keys.reshape(row_count, local_cols)
    d_values = d_values.reshape(row_count, local_cols)
    grad_b_qv = jnp.stack([jnp.sum(d_queries, axis=0), jnp.sum(d_values, axis=0)])
    stacked = jnp.stack([d_queries, d_keys, d_values]).astype(jnp.bfloat16)
    grad_w_qkv = jnp.einsum("td,stc->sdc", normed_one, stacked, preferred_element_type=jnp.float32)
    d_normed_one = mp_allreduce(
        jnp.einsum("stc,sdc->td", stacked, w_qkv, preferred_element_type=jnp.float32).astype(
            jnp.bfloat16
        ),
        n_mp,
    )
    d_input_norm, grad_ln1_gain, grad_ln1_bias = norm_one_back(d_normed_one)
    grad_tokens = d_middle + d_input_norm

    def scatter(grad, dim):
        return lax.psum_scatter(
            grad.astype(jnp.bfloat16), "dp", scatter_dimension=dim, tiled=True
        ).astype(jnp.float32)

    summed_qkv = scatter(grad_w_qkv, 1)
    summed_out = scatter(grad_w_out, 1)
    summed_fc1 = scatter(grad_w_fc1, 0)
    summed_fc2 = scatter(grad_w_fc2, 1)
    packed = jnp.concatenate(
        [
            grad_ln1_gain,
            grad_ln1_bias,
            grad_ln2_gain,
            grad_ln2_bias,
            grad_b_out,
            grad_b_fc2,
            grad_b_qv.reshape(-1),
            grad_b_fc1,
        ]
    )
    packed = lax.psum(packed, "dp")
    width = grad_ln1_gain.shape[0]
    pieces = [packed[k * width : (k + 1) * width] for k in range(6)]
    qv_size = grad_b_qv.size
    summed_b_qv = packed[6 * width : 6 * width + qv_size].reshape(grad_b_qv.shape)
    summed_b_fc1 = packed[6 * width + qv_size :]
    return (
        output,
        grad_tokens,
        summed_qkv,
        summed_b_qv,
        summed_out,
        pieces[4],
        summed_fc1,
        summed_b_fc1,
        summed_fc2,
        pieces[5],
        pieces[0],
        pieces[1],
        pieces[2],
        pieces[3],
    )


def solution(mesh):
    in_specs = (
        P("dp", None),
        P("dp", None),
        P("dp", None),
        P(None, None, "mp"),
        P(None, "mp"),
        P("mp", None),
        P(),
        P(None, "mp"),
        P("mp"),
        P("mp", None),
        P(),
        P(),
        P(),
        P(),
        P(),
    )
    out_specs = (
        P("dp", None),
        P("dp", None),
        P(None, "dp", "mp"),
        P(None, "mp"),
        P("mp", "dp"),
        P(),
        P("dp", "mp"),
        P("mp"),
        P("mp", "dp"),
        P(),
        P(),
        P(),
        P(),
        P(),
    )
    return jax.shard_map(
        partial(per_device, mesh.shape["mp"]),
        mesh=mesh,
        in_specs=in_specs,
        out_specs=out_specs,
        check_vma=False,
    )
```

profile of v0, /device:TPU:0, one launch (start us, length us, event | category | flops | bytes accessed | tf_op | source)
XLA Modules:
  0.0 817.9 jit_solution(1069003523429425183)
XLA Ops:
  32.4 64.2 %while.27 = (s32[]{:T(128)}, bf16[4,512,4,64]{1,3,2,0:T(8,128)(2,1)}, f32[4,4,512]{2,1,0:T(4,128)}, s32[4,512]{1,0:T(4,128)S(1)}, s32[2048]{0:T(1024)S(1)}, /*in...) while((s32[]{:T(128)}, ...), condition=%wide.region_7.8_spmd, body=%wide.region_4.7_spmd.sunk | while | flops 1125251072 | bytes 61421712 | solution.py:110
  117.3 45.9 %collective-permute-done.1 = bf16[1024,1024]{1,0:T(8,128)(2,1)S(1)} collective-permute-done((bf16[1024,1024]{1,0:T(8,128)(2,1)S(1)}, bf16[1024,1024]{1,0:T(8,128)(2,1)S(1)}, u32[]{:S(2)}, u32[]{:S(2)}) %collective-permute-start.1) | collective-permute-done | bytes 2097184 | tf_op jit(solution)/shard_map/ppermute | solution.py:38
  184.3 25.6 %fusion.103 = (f32[1024]{0:T(1024)}, bf16[2048,1024]{1,0:T(8,128)(2,1)}, f32[2048,1024]{1,0:T(8,128)}) fusion(f32[2048,1024]{1,0:T(8,128)S(1)} %fusion.100, f32[1024]{0:T(1024)S(1)} %copy-done.54, bf16[2048,1024]{1,0:T(8,128)(2,1)S(1)} %copy-done.22, bf16[1024,1024]{1,0:T(8,128)(2,1)S(1)} %copy-done), kind=kOutput, calls=%fused_computation.182 | convolution fusion | flops 4450155520 | bytes 27271168 | tf_op jit(solution)/shard_map/td,fd->tf/dot_general | solution.py:128
  209.8 10.1 %multiply_convert_fusion.1 = bf16[2048,1024]{1,0:T(8,128)(2,1)} fusion(f32[2048,1024]{1,0:T(8,128)} %get-tuple-element.335, f32[2048,1024]{1,0:T(8,128)} %copy-done.21, f32[1024]{0:T(1024)S(1)} %copy-done.54), kind=kLoop, calls=%fused_computation.86 | loop fusion | flops 8388608 | bytes 20975616 | tf_op jit(solution)/shard_map/convert_element_type | solution.py:120
  256.8 43.6 %collective-permute-done.7 = bf16[1024,1024]{1,0:T(8,128)(2,1)S(1)} collective-permute-done((bf16[1024,1024]{1,0:T(8,128)(2,1)S(1)}, bf16[1024,1024]{1,0:T(8,128)(2,1)S(1)}, u32[]{:S(2)}, u32[]{:S(2)}) %collective-permute-start.7) | collective-permute-done | bytes 2097184 | tf_op jit(solution)/shard_map/ppermute | solution.py:38
  302.7 11.1 %fusion.77 = bf16[1024,1024]{1,0:T(8,128)(2,1)} fusion(bf16[2048,1024]{1,0:T(8,128)(2,1)} %get-tuple-element.334, f32[1024]{0:T(1024)S(1)} %copy-done.57, f32[1024]{0:T(1024)S(1)} %copy-done.46, f32[2048]{0:T(1024)S(1)} %fusion.96, bf16[2048,1024]{1,0:T(8,128)(2,1)} %param.19, f32[2048]{0:T(1024)S(1)} %broadcast_multiply_fusion, f32[1024]{0:T(1024)S(1)} %copy-done.38, ...), kind=kOutput, calls=%fused_computation.142 | convolution fusion | flops 4321181696 | bytes 14708736 | tf_op jit(solution)/shard_map/td,tf->df/dot_general | solution.py:132
  314.0 30.5 %collective-permute-done.4 = bf16[1024,1024]{1,0:T(8,128)(2,1)} collective-permute-done((bf16[1024,1024]{1,0:T(8,128)(2,1)}, bf16[1024,1024]{1,0:T(8,128)(2,1)}, u32[]{:S(2)}, u32[]{:S(2)}) %collective-permute-start.4) | collective-permute-done | bytes 2097184 | tf_op jit(solution)/shard_map/ppermute | solution.py:38
  356.9 9.5 %fusion.57 = (f32[1024]{0:T(1024)}, f32[2048]{0:T(1024)S(1)}, f32[1024]{0:T(1024)}) fusion(f32[2048]{0:T(1024)S(1)} %fusion.96, bf16[1024,1024]{1,0:T(8,128)(2,1)S(1)} %get-tuple-element.347, bf16[1024,1024]{1,0:T(8,128)(2,1)S(1)} %get-tuple-element.346, f32[2048]{0:T(1024)S(1)} %broadcast_multiply_fusion, f32[1024]{0:T(1024)S(1)} %copy-done.38, ...), kind=kLoop, calls=%fused_computation.80 | loop fusion | flops 46133248 | bytes 12632064 | tf_op jit(solution)/shard_map/transpose(jvp())/reduce_sum | solution.py:15
  366.8 11.7 %fusion.105 = (f32[1024]{0:T(1024)}, f32[2048,1024]{1,0:T(8,128)S(1)}, bf16[2048,1024]{1,0:T(8,128)(2,1)}, f32[1024]{0:T(1024)}) fusion(f32[2048]{0:T(1024)S(1)} %negate_multiply_fusion.2, f32[2048]{0:T(1024)S(1)} %multiply_multiply_fusion.6, f32[2048]{0:T(1024)S(1)} %broadcast_multiply_fusion, f32[1024]{0:T(1024)S(1)} %copy-done.38, ...), kind=kLoop, calls=%fused_computation.183 | loop fusion | flops 60815360 | bytes 33607680 | tf_op jit(solution)/shard_map/reduce_sum | solution.py:141
  389.9 195.7 %while.28 = (s32[]{:T(128)}, f32[2048,4,64]{0,2,1:T(8,128)}, f32[2048,4,64]{0,2,1:T(8,128)}, f32[4,512,4,64]{1,3,2,0:T(8,128)}, bf16[4,512,4,64]{1,3,2,0:T(8,128...) while((s32[]{:T(128)}, f32[2048,4,64]{0,2,1:T(8,128)}, ...), condition=%wide.region_14.15_spmd.clone, body=%wide.region_12.14_spmd.clone.sunk | while | flops 2751068160 | bytes 164206880 | solution.py:179
  403.0 11.5 %multiply_reduce_fusion.3 = (f32[4,512]{1,0:T(4,128)}, f32[4,512,2048]{2,1,0:T(8,128)}) fusion(f32[4,512,2048]{2,1,0:T(8,128)S(1)} %fusion.167, f32[4,512]{1,0:T(4,128)S(1)} %dynamic-slice_bitcast_fusion.2, pred[512,2048]{1,0:T(8,128)(4,1)} %copy-done.8, bf16[2048,4,64]{0,2,1:T(8,128)(2,1)} %get-tuple-element.555, ...), kind=kOutput, calls=%fused_computation.19.clone.1 | convolution fusion | flops 557840384 | bytes 35930116 | tf_op jit(solution)/shard_map/while/body/eval_jaxpr/qhd,khd->hqk/dot_general | solution.py:154
  414.5 11.1 %multiply_convert_fusion.3 = bf16[4,512,2048]{2,1,0:T(8,128)(2,1)} fusion(f32[4,512,2048]{2,1,0:T(8,128)} %get-tuple-element.490, f32[4,512,2048]{2,1,0:T(8,128)S(1)} %fusion.167, f32[4,512]{1,0:T(4,128)} %get-tuple-element.491, f32[4,512]{1,0:T(4,128)S(1)} %dynamic-slice_bitcast_fusion.2, pred[512,2048]{1,0:T(8,128)(4,1)} %copy-done.8), kind=kLoop, calls=%fused_computation.18.clone.1 | loop fusion | flops 25165824 | bytes 43008000 | tf_op jit(solution)/shard_map/while/body/eval_jaxpr/convert_element_type | solution.py:158
  451.9 11.5 %multiply_reduce_fusion.3 = (f32[4,512]{1,0:T(4,128)}, f32[4,512,2048]{2,1,0:T(8,128)}) fusion(f32[4,512,2048]{2,1,0:T(8,128)S(1)} %fusion.167, f32[4,512]{1,0:T(4,128)S(1)} %dynamic-slice_bitcast_fusion.2, pred[512,2048]{1,0:T(8,128)(4,1)} %copy-done.8, bf16[2048,4,64]{0,2,1:T(8,128)(2,1)} %get-tuple-element.555, ...), kind=kOutput, calls=%fused_computation.19.clone.1 | convolution fusion | flops 557840384 | bytes 35930116 | tf_op jit(solution)/shard_map/while/body/eval_jaxpr/qhd,khd->hqk/dot_general | solution.py:154
  463.4 11.1 %multiply_convert_fusion.3 = bf16[4,512,2048]{2,1,0:T(8,128)(2,1)} fusion(f32[4,512,2048]{2,1,0:T(8,128)} %get-tuple-element.490, f32[4,512,2048]{2,1,0:T(8,128)S(1)} %fusion.167, f32[4,512]{1,0:T(4,128)} %get-tuple-element.491, f32[4,512]{1,0:T(4,128)S(1)} %dynamic-slice_bitcast_fusion.2, pred[512,2048]{1,0:T(8,128)(4,1)} %copy-done.8), kind=kLoop, calls=%fused_computation.18.clone.1 | loop fusion | flops 25165824 | bytes 43008000 | tf_op jit(solution)/shard_map/while/body/eval_jaxpr/convert_element_type | solution.py:158
  500.8 11.5 %multiply_reduce_fusion.3 = (f32[4,512]{1,0:T(4,128)}, f32[4,512,2048]{2,1,0:T(8,128)}) fusion(f32[4,512,2048]{2,1,0:T(8,128)S(1)} %fusion.167, f32[4,512]{1,0:T(4,128)S(1)} %dynamic-slice_bitcast_fusion.2, pred[512,2048]{1,0:T(8,128)(4,1)} %copy-done.8, bf16[2048,4,64]{0,2,1:T(8,128)(2,1)} %get-tuple-element.555, ...), kind=kOutput, calls=%fused_computation.19.clone.1 | convolution fusion | flops 557840384 | bytes 35930116 | tf_op jit(solution)/shard_map/while/body/eval_jaxpr/qhd,khd->hqk/dot_general | solution.py:154
  512.3 11.1 %multiply_convert_fusion.3 = bf16[4,512,2048]{2,1,0:T(8,128)(2,1)} fusion(f32[4,512,2048]{2,1,0:T(8,128)} %get-tuple-element.490, f32[4,512,2048]{2,1,0:T(8,128)S(1)} %fusion.167, f32[4,512]{1,0:T(4,128)} %get-tuple-element.491, f32[4,512]{1,0:T(4,128)S(1)} %dynamic-slice_bitcast_fusion.2, pred[512,2048]{1,0:T(8,128)(4,1)} %copy-done.8), kind=kLoop, calls=%fused_computation.18.clone.1 | loop fusion | flops 25165824 | bytes 43008000 | tf_op jit(solution)/shard_map/while/body/eval_jaxpr/convert_element_type | solution.py:158
  549.7 11.5 %multiply_reduce_fusion.3 = (f32[4,512]{1,0:T(4,128)}, f32[4,512,2048]{2,1,0:T(8,128)}) fusion(f32[4,512,2048]{2,1,0:T(8,128)S(1)} %fusion.167, f32[4,512]{1,0:T(4,128)S(1)} %dynamic-slice_bitcast_fusion.2, pred[512,2048]{1,0:T(8,128)(4,1)} %copy-done.8, bf16[2048,4,64]{0,2,1:T(8,128)(2,1)} %get-tuple-element.555, ...), kind=kOutput, calls=%fused_computation.19.clone.1 | convolution fusion | flops 557840384 | bytes 35930116 | tf_op jit(solution)/shard_map/while/body/eval_jaxpr/qhd,khd->hqk/dot_general | solution.py:154
  561.1 11.1 %multiply_convert_fusion.3 = bf16[4,512,2048]{2,1,0:T(8,128)(2,1)} fusion(f32[4,512,2048]{2,1,0:T(8,128)} %get-tuple-element.490, f32[4,512,2048]{2,1,0:T(8,128)S(1)} %fusion.167, f32[4,512]{1,0:T(4,128)} %get-tuple-element.491, f32[4,512]{1,0:T(4,128)S(1)} %dynamic-slice_bitcast_fusion.2, pred[512,2048]{1,0:T(8,128)(4,1)} %copy-done.8), kind=kLoop, calls=%fused_computation.18.clone.1 | loop fusion | flops 25165824 | bytes 43008000 | tf_op jit(solution)/shard_map/while/body/eval_jaxpr/convert_element_type | solution.py:158
  616.6 7.9 fusion.83
  632.0 25.2 %collective-permute-done.10 = bf16[1024,1024]{1,0:T(8,128)(2,1)} collective-permute-done((bf16[1024,1024]{1,0:T(8,128)(2,1)S(1)}, bf16[1024,1024]{1,0:T(8,128)(2,1)}, u32[]{:S(2)}, u32[]{:S(2)}) %collective-permute-start.10) | collective-permute-done | bytes 2097184 | tf_op jit(solution)/shard_map/ppermute | solution.py:38
  665.0 14.6 %reduce-scatter.15.cloned.1.call-done = bf16[128,256]{1,0:T(8,128)(2,1)} async-done(((bf16[1024,256]{1,0:T(8,128)(2,1)}), bf16[128,256]{1,0:T(8,128)(2,1)}) %reduce-scatter.15.cloned.1.call-update) | async-done | bytes 65552
  681.3 66.3 %reduce-scatter.13.cloned.1.call-done = bf16[128,768]{1,0:T(8,128)(2,1)} async-done(((bf16[1024,768]{1,0:T(8,128)(2,1)}), bf16[128,768]{1,0:T(8,128)(2,1)}) %reduce-scatter.13.cloned.1.call-update) | async-done | bytes 196624
  763.0 34.7 %psum.7 = f32[7680]{0:T(1024)S(1)} all-reduce(f32[7680]{0:T(1024)S(1)} %constant_dynamic-update-slice_fusion), channel_id=1, replica_groups=mesh['dp'=8,'mp'=4] {'dp'}, use_global_device_ids=true, to_apply=%region_27.28 | all-reduce | flops 7680 | bytes 61440 | tf_op jit(solution)/shard_map/psum | solution.py:218
  798.3 12.3 %add_add_fusion.2 = f32[2048,1024]{1,0:T(8,128)} fusion(f32[2048,1024]{1,0:T(8,128)} %copy-done.9, bf16[2048,1024]{1,0:T(8,128)(2,1)} %param.19, f32[2048]{0:T(1024)S(1)} %negate_multiply_fusion.1, f32[2048]{0:T(1024)S(1)} %multiply_multiply_fusion.5, f32[1024]{0:T(1024)S(1)} %copy-done.45, f32[2048]{0:T(1024)S(1)} %copy-done.37, f32[2048]{0:T(1024)S(1)} %copy-done.35, ...), kind=kLoop, calls=%fused_computation.83 | loop fusion | flops 27262976 | bytes 25202688 | tf_op jit(solution)/shard_map/add | solution.py:195
  (320 shorter events, 362.5 us)
Async XLA Ops:
  7.2 177.0 %copy-start = (bf16[1024,1024]{1,0:T(8,128)(2,1)S(1)}, bf16[1024,1024]{1,0:T(8,128)(2,1)}, u32[]{:S(2)}) copy-start(bf16[1024,1024]{1,0:T(8,128)(2,1)} %param.28) | copy-start | bytes 6291460
  7.2 653.9 %reduce-scatter.17.cloned.1.call-start = ((), (), s32[]{:S(2)}) async-start(), calls=%async_computation.7 | async-start | bytes 2359296
  106.5 4.7 collective-permute-start
  114.4 58.2 %copy-start.38 = (f32[1024]{0:T(1024)S(1)}, f32[1024]{0:T(1024)}, u32[]{:S(2)}) copy-start(f32[1024]{0:T(1024)} %param.25) | copy-start | bytes 12292
  114.4 48.9 %collective-permute-start.1 = (bf16[1024,1024]{1,0:T(8,128)(2,1)S(1)}, bf16[1024,1024]{1,0:T(8,128)(2,1)S(1)}, u32[]{:S(2)}, u32[]{:S(2)}) collective-permute-start(bf16[1024,1024]{1,0:T(8,128)(2,1)S(1)} %add_convert_fusion.9), channel_id=1, source_target_pairs={{0,2},{1,3},{2,0},{3,1},{4,6},{5,7},{6,4},{7,5},{8,10},{9,11},{10,... | collective-permute-start | bytes 6291464 | tf_op jit(solution)/shard_map/ppermute | solution.py:38
  165.5 4.5 collective-permute-start.2
  184.3 25.6 %copy-start.21 = (f32[2048,1024]{1,0:T(8,128)}, f32[2048,1024]{1,0:T(8,128)S(1)}, u32[]{:S(2)}) copy-start(f32[2048,1024]{1,0:T(8,128)S(1)} %fusion.100) | copy-start | bytes 25165828
  230.6 18.3 %collective-permute-start.6 = (bf16[1024,1024]{1,0:T(8,128)(2,1)}, bf16[1024,1024]{1,0:T(8,128)(2,1)}, u32[]{:S(2)}, u32[]{:S(2)}) collective-permute-start(bf16[1024,1024]{1,0:T(8,128)(2,1)} %constant_dynamic-slice_fusion.3), channel_id=1, source_target_pairs={{0,1},{1,0},{2,3},{3,2},{4,5},{5,4},{6,7},{7,6},{8,9},{9,8},{10,11... | collective-permute-start | bytes 6291464 | tf_op jit(solution)/shard_map/ppermute | solution.py:36
  240.6 422.5 %reduce-scatter.11.cloned.1.call-start = ((), (), s32[]{:S(2)}) async-start(), calls=%async_computation.4 | async-start | bytes 2359296 | tf_op jit(solution)/shard_map/reduce_scatter | solution.py:198
  248.5 54.2 %copy-start.13 = (bf16[1024,1024]{1,0:T(8,128)(2,1)S(1)}, bf16[1024,1024]{1,0:T(8,128)(2,1)}, u32[]{:S(2)}) copy-start(bf16[1024,1024]{1,0:T(8,128)(2,1)} %copy-done.12) | copy-start | bytes 6291460
  248.5 5.2 collective-permute-start.3
  251.9 48.6 %collective-permute-start.7 = (bf16[1024,1024]{1,0:T(8,128)(2,1)S(1)}, bf16[1024,1024]{1,0:T(8,128)(2,1)S(1)}, u32[]{:S(2)}, u32[]{:S(2)}) collective-permute-start(bf16[1024,1024]{1,0:T(8,128)(2,1)S(1)} %add_convert_fusion.5), channel_id=1, source_target_pairs={{0,2},{1,3},{2,0},{3,1},{4,6},{5,7},{6,4},{7,5},{8,10},{9,11},{10,... | collective-permute-start | bytes 6291464 | tf_op jit(solution)/shard_map/ppermute | solution.py:38
  256.0 88.6 %collective-permute-start.4 = (bf16[1024,1024]{1,0:T(8,128)(2,1)}, bf16[1024,1024]{1,0:T(8,128)(2,1)}, u32[]{:S(2)}, u32[]{:S(2)}) collective-permute-start(bf16[1024,1024]{1,0:T(8,128)(2,1)} %add_convert_fusion.7), channel_id=1, source_target_pairs={{0,2},{1,3},{2,0},{3,1},{4,6},{5,7},{6,4},{7,5},{8,10},{9,11},{10,... | collective-permute-start | bytes 6291464 | tf_op jit(solution)/shard_map/ppermute | solution.py:38
  302.7 45.2 %collective-permute-start.8 = (bf16[1024,1024]{1,0:T(8,128)(2,1)}, bf16[1024,1024]{1,0:T(8,128)(2,1)}, u32[]{:S(2)}, u32[]{:S(2)}) collective-permute-start(bf16[1024,1024]{1,0:T(8,128)(2,1)} %add_convert_fusion.4), channel_id=1, source_target_pairs={{0,1},{1,0},{2,3},{3,2},{4,5},{5,4},{6,7},{7,6},{8,9},{9,8},{10,11... | collective-permute-start | bytes 6291464 | tf_op jit(solution)/shard_map/ppermute | solution.py:40
  313.8 365.8 %reduce-scatter.15.cloned.1.call-start = ((), (), s32[]{:S(2)}) async-start(), calls=%async_computation.6 | async-start | bytes 589824
  314.0 36.5 %copy-start.4 = (bf16[2048,1024]{1,0:T(8,128)(2,1)S(1)}, bf16[2048,1024]{1,0:T(8,128)(2,1)}, u32[]{:S(2)}) copy-start(bf16[2048,1024]{1,0:T(8,128)(2,1)} %param.19) | copy-start | bytes 12582916
  314.0 36.5 %copy-start.15 = (bf16[1024,1024]{1,0:T(8,128)(2,1)S(1)}, bf16[1024,1024]{1,0:T(8,128)(2,1)}, u32[]{:S(2)}) copy-start(bf16[1024,1024]{1,0:T(8,128)(2,1)} %copy-done.14) | copy-start | bytes 6291460
  347.8 18.7 %collective-permute-start.5 = (bf16[1024,1024]{1,0:T(8,128)(2,1)S(1)}, bf16[1024,1024]{1,0:T(8,128)(2,1)S(1)}, u32[]{:S(2)}, u32[]{:S(2)}) collective-permute-start(bf16[1024,1024]{1,0:T(8,128)(2,1)S(1)} %add_convert_fusion.6), channel_id=1, source_target_pairs={{0,1},{1,0},{2,3},{3,2},{4,5},{5,4},{6,7},{7,6},{8,9},{9,8},{10,11... | collective-permute-start | bytes 6291464 | tf_op jit(solution)/shard_map/ppermute | solution.py:40
  603.8 4.3 collective-permute-start.9
  609.1 48.1 %collective-permute-start.10 = (bf16[1024,1024]{1,0:T(8,128)(2,1)S(1)}, bf16[1024,1024]{1,0:T(8,128)(2,1)}, u32[]{:S(2)}, u32[]{:S(2)}) collective-permute-start(bf16[1024,1024]{1,0:T(8,128)(2,1)S(1)} %add_convert_fusion.3), channel_id=1, source_target_pairs={{0,2},{1,3},{2,0},{3,1},{4,6},{5,7},{6,4},{7,5},{8,10},{9,11},{10,... | collective-permute-start | bytes 6291464 | tf_op jit(solution)/shard_map/ppermute | solution.py:38
  616.6 131.0 %reduce-scatter.13.cloned.1.call-start = ((), (), s32[]{:S(2)}) async-start(), calls=%async_computation.5 | async-start | bytes 1769472
  632.0 119.7 %copy-start.35 = (f32[2048]{0:T(1024)S(1)}, f32[2048]{0:T(1024)}, u32[]{:S(2)}) copy-start(f32[2048]{0:T(1024)} %copy-done.34) | copy-start | bytes 24580
  632.0 119.7 %copy-start.45 = (f32[1024]{0:T(1024)S(1)}, f32[1024]{0:T(1024)}, u32[]{:S(2)}) copy-start(f32[1024]{0:T(1024)} %param.30) | copy-start | bytes 12292
  661.1 88.6 %collective-permute-start.11 = (bf16[1024,1024]{1,0:T(8,128)(2,1)}, bf16[1024,1024]{1,0:T(8,128)(2,1)S(1)}, u32[]{:S(2)}, u32[]{:S(2)}) collective-permute-start(bf16[1024,1024]{1,0:T(8,128)(2,1)} %add_convert_fusion.2), channel_id=1, source_target_pairs={{0,1},{1,0},{2,3},{3,2},{4,5},{5,4},{6,7},{7,6},{8,9},{9,8},{10,11... | collective-permute-start | bytes 6291464 | tf_op jit(solution)/shard_map/ppermute | solution.py:40
  (65 other events, 488.7 us)
Sparse Core Ops, SparseCore 0:
  240.7 69.8 reduce-scatter.16
  314.1 69.8 reduce-scatter.10
  616.7 62.8 reduce-scatter.14
  682.9 64.5 reduce-scatter.12
where the time goes:
time: 828 us; the launch traced here: 818 us
  matrix products  276 us (33%)
  waiting for transfers between devices  239 us (29%)
  other arithmetic  182 us (22%)
  local copies, waits for them, and re-layouts  61.1 us (7%)
  blocking collectives  34.7 us (4%)
  between operations  14.9 us (2%)
  starting transfers between devices  9.39 us (1%)
    ppermute x4, waiting for transfers between devices, mp_allreduce(): got_far = lax.ppermute(first, 'mp', [(k, k ^ 2) for k in range(4)])  145 us
    unnamed x7, waiting for transfers between devices  81 us
    dot_general x4, matrix products, backward_block(): jnp.einsum('qhd,khd->hqk', d_out_block, value_heads, preferred_element_ty...  46 us
    convert_element_type x4, other arithmetic, backward_block(): d_scores_low = d_scores.astype(jnp.bfloat16)  44.5 us
    psum x1, blocking collectives, per_device(): packed = lax.psum(packed, 'dp')  34.7 us
    dot_general x8, matrix products, block_scores(): jnp.einsum('qhd,khd->hqk', query_block, key_heads, preferred_element_type...  31.8 us
    dot_general x4, matrix products, backward_block(): jnp.einsum('hqk,khd->qhd', d_scores_low, key_heads, preferred_element_typ...  30.6 us
    unnamed x125, local copies, waits for them, and re-layouts  30.4 us
  transfers between devices with their start and end apart: 16, of which 9 were waited for; matrix products, arithmetic and copies ran while one was open for 40% of the time, Pallas kernels for 0%

commit v1 on v0

--- a/solution.py
+++ b/solution.py
@@ -215,7 +215,7 @@
             grad_b_fc1,
         ]
     )
-    packed = lax.psum(packed, "dp")
+    packed = lax.all_gather(packed, "dp").sum(axis=0)
     width = grad_ln1_gain.shape[0]
     pieces = [packed[k * width : (k + 1) * width] for k in range(6)]
     qv_size = grad_b_qv.size

time: 828 us -> 825 us (level)
    psum x1 -> x0, blocking collectives: 34.7 us -> none  [per_device(): packed = lax.psum(packed, 'dp')]
    all_gather x0 -> x1, blocking collectives: none -> 30.7 us  [per_device(): packed = lax.all_gather(packed, 'dp').sum(axis=0)]
    unnamed x125 -> x126, local copies, waits for them, and re-layouts: 30.4 us -> 30.4 us
where the time goes in v1:
time: 825 us; the launch traced here: 814 us
  matrix products  276 us (33%)
  waiting for transfers between devices  239 us (29%)
  other arithmetic  182 us (22%)
  local copies, waits for them, and re-layouts  61.2 us (7%)
  blocking collectives  30.7 us (4%)
  between operations  15 us (2%)
  starting transfers between devices  9.39 us (1%)
    ppermute x4, waiting for transfers between devices, mp_allreduce(): got_far = lax.ppermute(first, 'mp', [(k, k ^ 2) for k in range(4)])  145 us
    unnamed x7, waiting for transfers between devices  81 us
    dot_general x4, matrix products, backward_block(): jnp.einsum('qhd,khd->hqk', d_out_block, value_heads, preferred_element_ty...  46 us
    convert_element_type x4, other arithmetic, backward_block(): d_scores_low = d_scores.astype(jnp.bfloat16)  44.5 us
    dot_general x8, matrix products, block_scores(): jnp.einsum('qhd,khd->hqk', query_block, key_heads, preferred_element_type...  31.8 us
    all_gather x1, blocking collectives, per_device(): packed = lax.all_gather(packed, 'dp').sum(axis=0)  30.7 us
    dot_general x4, matrix products, backward_block(): jnp.einsum('hqk,khd->qhd', d_scores_low, key_heads, preferred_element_typ...  30.6 us
    unnamed x126, local copies, waits for them, and re-layouts  30.4 us
  transfers between devices with their start and end apart: 16, of which 9 were waited for; matrix products, arithmetic and copies ran while one was open for 40% of the time, Pallas kernels for 0%

profile of v1, /device:TPU:0, one launch (start us, length us, event | category | flops | bytes accessed | tf_op | source)
XLA Modules:
  0.0 814.2 jit_solution(3464498612069114334)
XLA Ops:
  32.4 64.2 %while.27 = (s32[]{:T(128)}, bf16[4,512,4,64]{1,3,2,0:T(8,128)(2,1)}, f32[4,4,512]{2,1,0:T(4,128)}, s32[4,512]{1,0:T(4,128)S(1)}, s32[2048]{0:T(1024)S(1)}, /*in...) while((s32[]{:T(128)}, ...), condition=%wide.region_7.8_spmd, body=%wide.region_4.7_spmd.sunk | while | flops 1125251072 | bytes 61421712 | solution.py:110
  117.3 45.9 %collective-permute-done.1 = bf16[1024,1024]{1,0:T(8,128)(2,1)S(1)} collective-permute-done((bf16[1024,1024]{1,0:T(8,128)(2,1)S(1)}, bf16[1024,1024]{1,0:T(8,128)(2,1)S(1)}, u32[]{:S(2)}, u32[]{:S(2)}) %collective-permute-start.1) | collective-permute-done | bytes 2097184 | tf_op jit(solution)/shard_map/ppermute | solution.py:38
  184.3 25.6 %fusion.103 = (f32[1024]{0:T(1024)}, bf16[2048,1024]{1,0:T(8,128)(2,1)}, f32[2048,1024]{1,0:T(8,128)}) fusion(f32[2048,1024]{1,0:T(8,128)S(1)} %fusion.100, f32[1024]{0:T(1024)S(1)} %copy-done.54, bf16[2048,1024]{1,0:T(8,128)(2,1)S(1)} %copy-done.22, bf16[1024,1024]{1,0:T(8,128)(2,1)S(1)} %copy-done), kind=kOutput, calls=%fused_computation.182 | convolution fusion | flops 4450155520 | bytes 27271168 | tf_op jit(solution)/shard_map/td,fd->tf/dot_general | solution.py:128
  209.8 10.1 %multiply_convert_fusion.1 = bf16[2048,1024]{1,0:T(8,128)(2,1)} fusion(f32[2048,1024]{1,0:T(8,128)} %get-tuple-element.335, f32[2048,1024]{1,0:T(8,128)} %copy-done.21, f32[1024]{0:T(1024)S(1)} %copy-done.54), kind=kLoop, calls=%fused_computation.86 | loop fusion | flops 8388608 | bytes 20975616 | tf_op jit(solution)/shard_map/convert_element_type | solution.py:120
  256.8 43.6 %collective-permute-done.7 = bf16[1024,1024]{1,0:T(8,128)(2,1)S(1)} collective-permute-done((bf16[1024,1024]{1,0:T(8,128)(2,1)S(1)}, bf16[1024,1024]{1,0:T(8,128)(2,1)S(1)}, u32[]{:S(2)}, u32[]{:S(2)}) %collective-permute-start.7) | collective-permute-done | bytes 2097184 | tf_op jit(solution)/shard_map/ppermute | solution.py:38
  302.7 11.1 %fusion.77 = bf16[1024,1024]{1,0:T(8,128)(2,1)} fusion(bf16[2048,1024]{1,0:T(8,128)(2,1)} %get-tuple-element.334, f32[1024]{0:T(1024)S(1)} %copy-done.57, f32[1024]{0:T(1024)S(1)} %copy-done.46, f32[2048]{0:T(1024)S(1)} %fusion.96, bf16[2048,1024]{1,0:T(8,128)(2,1)} %param.19, f32[2048]{0:T(1024)S(1)} %broadcast_multiply_fusion, f32[1024]{0:T(1024)S(1)} %copy-done.38, ...), kind=kOutput, calls=%fused_computation.142 | convolution fusion | flops 4321181696 | bytes 14708736 | tf_op jit(solution)/shard_map/td,tf->df/dot_general | solution.py:132
  314.0 30.5 %collective-permute-done.4 = bf16[1024,1024]{1,0:T(8,128)(2,1)} collective-permute-done((bf16[1024,1024]{1,0:T(8,128)(2,1)}, bf16[1024,1024]{1,0:T(8,128)(2,1)}, u32[]{:S(2)}, u32[]{:S(2)}) %collective-permute-start.4) | collective-permute-done | bytes 2097184 | tf_op jit(solution)/shard_map/ppermute | solution.py:38
  356.9 9.5 %fusion.57 = (f32[1024]{0:T(1024)}, f32[2048]{0:T(1024)S(1)}, f32[1024]{0:T(1024)}) fusion(f32[2048]{0:T(1024)S(1)} %fusion.96, bf16[1024,1024]{1,0:T(8,128)(2,1)S(1)} %get-tuple-element.347, bf16[1024,1024]{1,0:T(8,128)(2,1)S(1)} %get-tuple-element.346, f32[2048]{0:T(1024)S(1)} %broadcast_multiply_fusion, f32[1024]{0:T(1024)S(1)} %copy-done.38, ...), kind=kLoop, calls=%fused_computation.80 | loop fusion | flops 46133248 | bytes 12632064 | tf_op jit(solution)/shard_map/transpose(jvp())/reduce_sum | solution.py:15
  366.8 11.7 %fusion.105 = (f32[1024]{0:T(1024)}, f32[2048,1024]{1,0:T(8,128)S(1)}, bf16[2048,1024]{1,0:T(8,128)(2,1)}, f32[1024]{0:T(1024)}) fusion(f32[2048]{0:T(1024)S(1)} %negate_multiply_fusion.2, f32[2048]{0:T(1024)S(1)} %multiply_multiply_fusion.6, f32[2048]{0:T(1024)S(1)} %broadcast_multiply_fusion, f32[1024]{0:T(1024)S(1)} %copy-done.38, ...), kind=kLoop, calls=%fused_computation.183 | loop fusion | flops 60815360 | bytes 33607680 | tf_op jit(solution)/shard_map/reduce_sum | solution.py:141
  389.9 195.7 %while.28 = (s32[]{:T(128)}, f32[2048,4,64]{0,2,1:T(8,128)}, f32[2048,4,64]{0,2,1:T(8,128)}, f32[4,512,4,64]{1,3,2,0:T(8,128)}, bf16[4,512,4,64]{1,3,2,0:T(8,128...) while((s32[]{:T(128)}, f32[2048,4,64]{0,2,1:T(8,128)}, ...), condition=%wide.region_14.15_spmd.clone, body=%wide.region_12.14_spmd.clone.sunk | while | flops 2751068160 | bytes 164206880 | solution.py:179
  403.0 11.5 %multiply_reduce_fusion.3 = (f32[4,512]{1,0:T(4,128)}, f32[4,512,2048]{2,1,0:T(8,128)}) fusion(f32[4,512,2048]{2,1,0:T(8,128)S(1)} %fusion.167, f32[4,512]{1,0:T(4,128)S(1)} %dynamic-slice_bitcast_fusion.2, pred[512,2048]{1,0:T(8,128)(4,1)} %copy-done.8, bf16[2048,4,64]{0,2,1:T(8,128)(2,1)} %get-tuple-element.555, ...), kind=kOutput, calls=%fused_computation.19.clone.1 | convolution fusion | flops 557840384 | bytes 35930116 | tf_op jit(solution)/shard_map/while/body/eval_jaxpr/qhd,khd->hqk/dot_general | solution.py:154
  414.5 11.1 %multiply_convert_fusion.3 = bf16[4,512,2048]{2,1,0:T(8,128)(2,1)} fusion(f32[4,512,2048]{2,1,0:T(8,128)} %get-tuple-element.490, f32[4,512,2048]{2,1,0:T(8,128)S(1)} %fusion.167, f32[4,512]{1,0:T(4,128)} %get-tuple-element.491, f32[4,512]{1,0:T(4,128)S(1)} %dynamic-slice_bitcast_fusion.2, pred[512,2048]{1,0:T(8,128)(4,1)} %copy-done.8), kind=kLoop, calls=%fused_computation.18.clone.1 | loop fusion | flops 25165824 | bytes 43008000 | tf_op jit(solution)/shard_map/while/body/eval_jaxpr/convert_element_type | solution.py:158
  451.9 11.5 %multiply_reduce_fusion.3 = (f32[4,512]{1,0:T(4,128)}, f32[4,512,2048]{2,1,0:T(8,128)}) fusion(f32[4,512,2048]{2,1,0:T(8,128)S(1)} %fusion.167, f32[4,512]{1,0:T(4,128)S(1)} %dynamic-slice_bitcast_fusion.2, pred[512,2048]{1,0:T(8,128)(4,1)} %copy-done.8, bf16[2048,4,64]{0,2,1:T(8,128)(2,1)} %get-tuple-element.555, ...), kind=kOutput, calls=%fused_computation.19.clone.1 | convolution fusion | flops 557840384 | bytes 35930116 | tf_op jit(solution)/shard_map/while/body/eval_jaxpr/qhd,khd->hqk/dot_general | solution.py:154
  463.4 11.1 %multiply_convert_fusion.3 = bf16[4,512,2048]{2,1,0:T(8,128)(2,1)} fusion(f32[4,512,2048]{2,1,0:T(8,128)} %get-tuple-element.490, f32[4,512,2048]{2,1,0:T(8,128)S(1)} %fusion.167, f32[4,512]{1,0:T(4,128)} %get-tuple-element.491, f32[4,512]{1,0:T(4,128)S(1)} %dynamic-slice_bitcast_fusion.2, pred[512,2048]{1,0:T(8,128)(4,1)} %copy-done.8), kind=kLoop, calls=%fused_computation.18.clone.1 | loop fusion | flops 25165824 | bytes 43008000 | tf_op jit(solution)/shard_map/while/body/eval_jaxpr/convert_element_type | solution.py:158
  500.8 11.5 %multiply_reduce_fusion.3 = (f32[4,512]{1,0:T(4,128)}, f32[4,512,2048]{2,1,0:T(8,128)}) fusion(f32[4,512,2048]{2,1,0:T(8,128)S(1)} %fusion.167, f32[4,512]{1,0:T(4,128)S(1)} %dynamic-slice_bitcast_fusion.2, pred[512,2048]{1,0:T(8,128)(4,1)} %copy-done.8, bf16[2048,4,64]{0,2,1:T(8,128)(2,1)} %get-tuple-element.555, ...), kind=kOutput, calls=%fused_computation.19.clone.1 | convolution fusion | flops 557840384 | bytes 35930116 | tf_op jit(solution)/shard_map/while/body/eval_jaxpr/qhd,khd->hqk/dot_general | solution.py:154
  512.3 11.1 %multiply_convert_fusion.3 = bf16[4,512,2048]{2,1,0:T(8,128)(2,1)} fusion(f32[4,512,2048]{2,1,0:T(8,128)} %get-tuple-element.490, f32[4,512,2048]{2,1,0:T(8,128)S(1)} %fusion.167, f32[4,512]{1,0:T(4,128)} %get-tuple-element.491, f32[4,512]{1,0:T(4,128)S(1)} %dynamic-slice_bitcast_fusion.2, pred[512,2048]{1,0:T(8,128)(4,1)} %copy-done.8), kind=kLoop, calls=%fused_computation.18.clone.1 | loop fusion | flops 25165824 | bytes 43008000 | tf_op jit(solution)/shard_map/while/body/eval_jaxpr/convert_element_type | solution.py:158
  549.7 11.5 %multiply_reduce_fusion.3 = (f32[4,512]{1,0:T(4,128)}, f32[4,512,2048]{2,1,0:T(8,128)}) fusion(f32[4,512,2048]{2,1,0:T(8,128)S(1)} %fusion.167, f32[4,512]{1,0:T(4,128)S(1)} %dynamic-slice_bitcast_fusion.2, pred[512,2048]{1,0:T(8,128)(4,1)} %copy-done.8, bf16[2048,4,64]{0,2,1:T(8,128)(2,1)} %get-tuple-element.555, ...), kind=kOutput, calls=%fused_computation.19.clone.1 | convolution fusion | flops 557840384 | bytes 35930116 | tf_op jit(solution)/shard_map/while/body/eval_jaxpr/qhd,khd->hqk/dot_general | solution.py:154
  561.1 11.1 %multiply_convert_fusion.3 = bf16[4,512,2048]{2,1,0:T(8,128)(2,1)} fusion(f32[4,512,2048]{2,1,0:T(8,128)} %get-tuple-element.490, f32[4,512,2048]{2,1,0:T(8,128)S(1)} %fusion.167, f32[4,512]{1,0:T(4,128)} %get-tuple-element.491, f32[4,512]{1,0:T(4,128)S(1)} %dynamic-slice_bitcast_fusion.2, pred[512,2048]{1,0:T(8,128)(4,1)} %copy-done.8), kind=kLoop, calls=%fused_computation.18.clone.1 | loop fusion | flops 25165824 | bytes 43008000 | tf_op jit(solution)/shard_map/while/body/eval_jaxpr/convert_element_type | solution.py:158
  616.6 7.9 fusion.83
  632.0 25.2 %collective-permute-done.10 = bf16[1024,1024]{1,0:T(8,128)(2,1)} collective-permute-done((bf16[1024,1024]{1,0:T(8,128)(2,1)S(1)}, bf16[1024,1024]{1,0:T(8,128)(2,1)}, u32[]{:S(2)}, u32[]{:S(2)}) %collective-permute-start.10) | collective-permute-done | bytes 2097184 | tf_op jit(solution)/shard_map/ppermute | solution.py:38
  665.0 14.6 %reduce-scatter.15.cloned.1.call-done = bf16[128,256]{1,0:T(8,128)(2,1)} async-done(((bf16[1024,256]{1,0:T(8,128)(2,1)}), bf16[128,256]{1,0:T(8,128)(2,1)}) %reduce-scatter.15.cloned.1.call-update) | async-done | bytes 65552
  681.3 66.3 %reduce-scatter.13.cloned.1.call-done = bf16[128,768]{1,0:T(8,128)(2,1)} async-done(((bf16[1024,768]{1,0:T(8,128)(2,1)}), bf16[128,768]{1,0:T(8,128)(2,1)}) %reduce-scatter.13.cloned.1.call-update) | async-done | bytes 196624
  763.0 30.7 %all-gather.1 = f32[8,1,7680]{2,1,0:T(1,128)S(1)} all-gather(f32[1,1,7680]{2,1,0:T(1,128)S(1)} %reshape.251), channel_id=2, replica_groups=mesh['dp'=8,'mp'=4] {'dp'}, dimensions={0}, use_global_device_ids=true | all-gather | bytes 276480 | tf_op jit(solution)/shard_map/all_gather | solution.py:218
  794.6 12.3 %add_add_fusion.2 = f32[2048,1024]{1,0:T(8,128)} fusion(f32[2048,1024]{1,0:T(8,128)} %copy-done.9, bf16[2048,1024]{1,0:T(8,128)(2,1)} %param.19, f32[2048]{0:T(1024)S(1)} %negate_multiply_fusion.1, f32[2048]{0:T(1024)S(1)} %multiply_multiply_fusion.5, f32[1024]{0:T(1024)S(1)} %copy-done.45, f32[2048]{0:T(1024)S(1)} %copy-done.37, f32[2048]{0:T(1024)S(1)} %copy-done.35, ...), kind=kLoop, calls=%fused_computation.83 | loop fusion | flops 27262976 | bytes 25202688 | tf_op jit(solution)/shard_map/add | solution.py:195
  (322 shorter events, 362.7 us)
Async XLA Ops:
  7.2 177.0 %copy-start = (bf16[1024,1024]{1,0:T(8,128)(2,1)S(1)}, bf16[1024,1024]{1,0:T(8,128)(2,1)}, u32[]{:S(2)}) copy-start(bf16[1024,1024]{1,0:T(8,128)(2,1)} %param.28) | copy-start | bytes 6291460
  7.2 653.9 %reduce-scatter.17.cloned.1.call-start = ((), (), s32[]{:S(2)}) async-start(), calls=%async_computation.7 | async-start | bytes 2359296
  106.5 4.7 collective-permute-start
  114.4 58.2 %copy-start.38 = (f32[1024]{0:T(1024)S(1)}, f32[1024]{0:T(1024)}, u32[]{:S(2)}) copy-start(f32[1024]{0:T(1024)} %param.25) | copy-start | bytes 12292
  114.4 48.9 %collective-permute-start.1 = (bf16[1024,1024]{1,0:T(8,128)(2,1)S(1)}, bf16[1024,1024]{1,0:T(8,128)(2,1)S(1)}, u32[]{:S(2)}, u32[]{:S(2)}) collective-permute-start(bf16[1024,1024]{1,0:T(8,128)(2,1)S(1)} %add_convert_fusion.9), channel_id=1, source_target_pairs={{0,2},{1,3},{2,0},{3,1},{4,6},{5,7},{6,4},{7,5},{8,10},{9,11},{10,... | collective-permute-start | bytes 6291464 | tf_op jit(solution)/shard_map/ppermute | solution.py:38
  165.5 4.5 collective-permute-start.2
  184.3 25.6 %copy-start.21 = (f32[2048,1024]{1,0:T(8,128)}, f32[2048,1024]{1,0:T(8,128)S(1)}, u32[]{:S(2)}) copy-start(f32[2048,1024]{1,0:T(8,128)S(1)} %fusion.100) | copy-start | bytes 25165828
  230.6 18.3 %collective-permute-start.6 = (bf16[1024,1024]{1,0:T(8,128)(2,1)}, bf16[1024,1024]{1,0:T(8,128)(2,1)}, u32[]{:S(2)}, u32[]{:S(2)}) collective-permute-start(bf16[1024,1024]{1,0:T(8,128)(2,1)} %constant_dynamic-slice_fusion.3), channel_id=1, source_target_pairs={{0,1},{1,0},{2,3},{3,2},{4,5},{5,4},{6,7},{7,6},{8,9},{9,8},{10,11... | collective-permute-start | bytes 6291464 | tf_op jit(solution)/shard_map/ppermute | solution.py:36
  240.6 422.5 %reduce-scatter.11.cloned.1.call-start = ((), (), s32[]{:S(2)}) async-start(), calls=%async_computation.4 | async-start | bytes 2359296 | tf_op jit(solution)/shard_map/reduce_scatter | solution.py:198
  248.5 54.2 %copy-start.13 = (bf16[1024,1024]{1,0:T(8,128)(2,1)S(1)}, bf16[1024,1024]{1,0:T(8,128)(2,1)}, u32[]{:S(2)}) copy-start(bf16[1024,1024]{1,0:T(8,128)(2,1)} %copy-done.12) | copy-start | bytes 6291460
  248.5 5.2 collective-permute-start.3
  251.9 48.6 %collective-permute-start.7 = (bf16[1024,1024]{1,0:T(8,128)(2,1)S(1)}, bf16[1024,1024]{1,0:T(8,128)(2,1)S(1)}, u32[]{:S(2)}, u32[]{:S(2)}) collective-permute-start(bf16[1024,1024]{1,0:T(8,128)(2,1)S(1)} %add_convert_fusion.5), channel_id=1, source_target_pairs={{0,2},{1,3},{2,0},{3,1},{4,6},{5,7},{6,4},{7,5},{8,10},{9,11},{10,... | collective-permute-start | bytes 6291464 | tf_op jit(solution)/shard_map/ppermute | solution.py:38
  256.0 88.6 %collective-permute-start.4 = (bf16[1024,1024]{1,0:T(8,128)(2,1)}, bf16[1024,1024]{1,0:T(8,128)(2,1)}, u32[]{:S(2)}, u32[]{:S(2)}) collective-permute-start(bf16[1024,1024]{1,0:T(8,128)(2,1)} %add_convert_fusion.7), channel_id=1, source_target_pairs={{0,2},{1,3},{2,0},{3,1},{4,6},{5,7},{6,4},{7,5},{8,10},{9,11},{10,... | collective-permute-start | bytes 6291464 | tf_op jit(solution)/shard_map/ppermute | solution.py:38
  302.7 45.2 %collective-permute-start.8 = (bf16[1024,1024]{1,0:T(8,128)(2,1)}, bf16[1024,1024]{1,0:T(8,128)(2,1)}, u32[]{:S(2)}, u32[]{:S(2)}) collective-permute-start(bf16[1024,1024]{1,0:T(8,128)(2,1)} %add_convert_fusion.4), channel_id=1, source_target_pairs={{0,1},{1,0},{2,3},{3,2},{4,5},{5,4},{6,7},{7,6},{8,9},{9,8},{10,11... | collective-permute-start | bytes 6291464 | tf_op jit(solution)/shard_map/ppermute | solution.py:40
  313.8 365.8 %reduce-scatter.15.cloned.1.call-start = ((), (), s32[]{:S(2)}) async-start(), calls=%async_computation.6 | async-start | bytes 589824
  314.0 36.5 %copy-start.4 = (bf16[2048,1024]{1,0:T(8,128)(2,1)S(1)}, bf16[2048,1024]{1,0:T(8,128)(2,1)}, u32[]{:S(2)}) copy-start(bf16[2048,1024]{1,0:T(8,128)(2,1)} %param.19) | copy-start | bytes 12582916
  314.0 36.5 %copy-start.15 = (bf16[1024,1024]{1,0:T(8,128)(2,1)S(1)}, bf16[1024,1024]{1,0:T(8,128)(2,1)}, u32[]{:S(2)}) copy-start(bf16[1024,1024]{1,0:T(8,128)(2,1)} %copy-done.14) | copy-start | bytes 6291460
  347.8 18.7 %collective-permute-start.5 = (bf16[1024,1024]{1,0:T(8,128)(2,1)S(1)}, bf16[1024,1024]{1,0:T(8,128)(2,1)S(1)}, u32[]{:S(2)}, u32[]{:S(2)}) collective-permute-start(bf16[1024,1024]{1,0:T(8,128)(2,1)S(1)} %add_convert_fusion.6), channel_id=1, source_target_pairs={{0,1},{1,0},{2,3},{3,2},{4,5},{5,4},{6,7},{7,6},{8,9},{9,8},{10,11... | collective-permute-start | bytes 6291464 | tf_op jit(solution)/shard_map/ppermute | solution.py:40
  603.8 4.3 collective-permute-start.9
  609.1 48.1 %collective-permute-start.10 = (bf16[1024,1024]{1,0:T(8,128)(2,1)S(1)}, bf16[1024,1024]{1,0:T(8,128)(2,1)}, u32[]{:S(2)}, u32[]{:S(2)}) collective-permute-start(bf16[1024,1024]{1,0:T(8,128)(2,1)S(1)} %add_convert_fusion.3), channel_id=1, source_target_pairs={{0,2},{1,3},{2,0},{3,1},{4,6},{5,7},{6,4},{7,5},{8,10},{9,11},{10,... | collective-permute-start | bytes 6291464 | tf_op jit(solution)/shard_map/ppermute | solution.py:38
  616.6 131.0 %reduce-scatter.13.cloned.1.call-start = ((), (), s32[]{:S(2)}) async-start(), calls=%async_computation.5 | async-start | bytes 1769472
  632.0 119.7 %copy-start.35 = (f32[2048]{0:T(1024)S(1)}, f32[2048]{0:T(1024)}, u32[]{:S(2)}) copy-start(f32[2048]{0:T(1024)} %copy-done.34) | copy-start | bytes 24580
  632.0 119.7 %copy-start.45 = (f32[1024]{0:T(1024)S(1)}, f32[1024]{0:T(1024)}, u32[]{:S(2)}) copy-start(f32[1024]{0:T(1024)} %param.30) | copy-start | bytes 12292
  661.1 88.6 %collective-permute-start.11 = (bf16[1024,1024]{1,0:T(8,128)(2,1)}, bf16[1024,1024]{1,0:T(8,128)(2,1)S(1)}, u32[]{:S(2)}, u32[]{:S(2)}) collective-permute-start(bf16[1024,1024]{1,0:T(8,128)(2,1)} %add_convert_fusion.2), channel_id=1, source_target_pairs={{0,1},{1,0},{2,3},{3,2},{4,5},{5,4},{6,7},{7,6},{8,9},{9,8},{10,11... | collective-permute-start | bytes 6291464 | tf_op jit(solution)/shard_map/ppermute | solution.py:40
  (65 other events, 488.7 us)
Sparse Core Ops, SparseCore 0:
  240.7 69.8 reduce-scatter.16
  314.1 69.8 reduce-scatter.10
  616.7 62.8 reduce-scatter.14
  682.9 64.5 reduce-scatter.12
